TPU v7x, 32 devices: a whole 2x2x4 slice. The times are simulated.
32 devices in a mesh: items: 8 (over z, y), users: 4 (over x, core).
Axes of the slice: x: 2, y: 2, z: 4, core: 2. Of those that a mesh axis runs over, the one named last changes fastest.
Arguments:
- user_emb: bfloat16 [4096, 256], P('users', 'items'), as said below
- item_emb: bfloat16 [262144, 256], P('items'), as said below
- target: int32 [4096], P('users'), may hold values from 0 to 262143
- history: int32 [4096, 32], P('users'), may hold values from 0 to 262143, as said below
Outputs:
- log_rank: float32 [4096], P('users')
- metrics: float32 [2], replicated
Inputs may be any that keep to these rules, and one draw needn't show every extreme that they name: history[u, k] lies in [k * 8192, (k + 1) * 8192); a user's history entries are thus distinct. `item_emb`: rows of norm about one. `user_emb`: entries of order one.
All inputs are finite; a program needn't handle non-finite values.
Results may differ from a plain program's by a relative error of at most 0.0003.
Values may be sent and summed in bfloat16 or wider, within the bound.
A program may use at most 64 MiB of HBM per device.

v0:
```python
import jax
import jax.numpy as jnp
from jax import lax
from jax.sharding import PartitionSpec as P

sharpness = 4.0


def body(user_emb, item_emb, target, history):
    item_dev = item_emb.shape[0]
    shard = lax.axis_index("items")
    start = shard * item_dev
    local_t = target - start
    inside = (local_t >= 0) & (local_t < item_dev)
    own_rows = item_emb[jnp.clip(local_t, 0, item_dev - 1)]
    users = lax.all_gather(user_emb, "items", axis=1, tiled=True)
    partial_t = jnp.sum(users.astype(jnp.float32) * own_rows.astype(jnp.float32), axis=1)
    tscore = lax.psum(jnp.where(inside, partial_t, 0.0), "items")
    n_items = lax.axis_size("items")
    n_users = lax.axis_size("users")
    u_dev = users.shape[0]
    blk = min(item_dev, 4096)
    nblk = item_dev // blk

    def add_block(index, total):
        rows = lax.dynamic_slice_in_dim(item_emb, index * blk, blk, 0)
        score = lax.dot_general(
            users, rows, (((1,), (1,)), ((), ())), preferred_element_type=jnp.float32
        )
        return total + jnp.sum(jax.nn.sigmoid(sharpness * (score - tscore[:, None])), axis=1)

    total = lax.fori_loop(0, nblk, add_block, jnp.zeros((u_dev,), jnp.float32))
    per_shard = history.shape[1] // n_items
    own_hist = lax.dynamic_slice_in_dim(history, shard * per_shard, per_shard, 1)
    hrows = item_emb[own_hist - start]
    hscore = jnp.einsum("ud,uhd->uh", users, hrows, preferred_element_type=jnp.float32)
    local = total - jnp.sum(jax.nn.sigmoid(sharpness * (hscore - tscore[:, None])), axis=1)
    seen = jnp.any(history == target[:, None], axis=1)
    correction = jnp.where(seen, 0.0, 0.5).astype(jnp.float32)
    all_users = u_dev * n_users
    above = lax.psum(local, "items") - correction
    rank = 1.0 + above
    log_rank = jnp.log(rank)
    hit = jax.nn.sigmoid(10.5 - rank)
    gain = hit / jnp.log2(1.0 + rank)
    hit_sum, gain_sum = lax.psum((jnp.sum(hit), jnp.sum(gain)), "users")
    metrics = jnp.stack([hit_sum, gain_sum]) / all_users
    return (log_rank, metrics)


def solution(mesh):
    return jax.shard_map(
        body,
        mesh=mesh,
        in_specs=(P("users", "items"), P("items", None), P("users"), P("users", None)),
        out_specs=(P("users"), P()),
        check_vma=False,
    )
```

profile of v0, /device:TPU:0, one launch (start us, length us, event | category | flops | bytes accessed | tf_op | source)
XLA Modules:
  0.0 174.1 jit_solution(5118468006411309888)
XLA Ops:
  0.6 0.0 copy-start.1
  0.6 0.0 copy-start.2
  0.7 0.8 compare_select_fusion
  1.5 0.2 copy.14
  1.7 0.3 reshape.17
  2.0 20.9 %gather_fusion.1 = bf16[4096,256]{1,0:T(8,128)(2,1)S(1)} fusion(bf16[32768,256]{1,0:T(8,128)(2,1)} %param.7, s32[4096]{0:T(1024)S(1)} %broadcast_clamp_fusion), kind=kCustom, calls=%fused_computation.1 | custom fusion | bytes 4210688 | tf_op jit(solution)/shard_map/gather | solution.py:35
  22.9 2.1 %reshape.16 = bf16[1024,4,256]{2,1,0:T(4,128)(2,1)} reshape(bf16[4096,256]{1,0:T(8,128)(2,1)S(1)} %gather_fusion.1) | data formatting | bytes 4194304 | tf_op jit(solution)/shard_map/gather | solution.py:35
  25.0 0.0 copy-done.1
  25.0 33.0 %all_gather.3 = bf16[1024,256]{0,1:T(8,128)(2,1)S(1)} all-gather(bf16[1024,32]{0,1:T(8,128)(2,1)S(1)} %copy-done.1), channel_id=1, replica_groups=mesh['items'=8,'users'=4] {'items'}, dimensions={1}, use_global_device_ids=true | all-gather | bytes 589824 | tf_op jit(solution)/shard_map/all_gather | solution.py:16
  58.0 0.2 copy.20
  58.2 2.9 %multiply_reduce_fusion = f32[1024,4]{1,0:T(8,128)S(1)} fusion(f32[1024,256]{1,0:T(8,128)S(1)} %copy.20, bf16[1024,4,256]{2,1,0:T(4,128)(2,1)} %reshape.16), kind=kLoop, calls=%fused_computation.7 | loop fusion | flops 3141632 | bytes 3162112
  61.1 0.2 copy.19
  61.3 0.0 copy-done.2
  61.3 11.4 %gather_fusion = bf16[1024,256]{1,0:T(8,128)(2,1)S(1)} fusion(bf16[32768,256]{1,0:T(8,128)(2,1)} %param.7, s32[1024]{0:T(1024)S(1)} %fusion.4), kind=kCustom, calls=%fused_computation | custom fusion | bytes 1052672 | tf_op jit(solution)/shard_map/gather | solution.py:15
  72.7 0.2 copy.13
  73.0 0.2 multiply_reduce_fusion.1
  73.2 21.5 %psum.28 = f32[1024]{0:T(1024)S(1)} all-reduce(f32[1024]{0:T(1024)S(1)} %and_select_fusion), channel_id=1, replica_groups=mesh['items'=8,'users'=4] {'items'}, use_global_device_ids=true, to_apply=%region_1.2 | all-reduce | flops 1024 | bytes 8192 | tf_op jit(solution)/shard_map/psum | solution.py:18
  94.8 0.0 copy-start
  94.8 52.7 %while.14 = (s32[]{:T(128)}, f32[1024]{0:T(1024)S(1)}, bf16[32768,256]{1,0:T(8,128)(2,1)}, bf16[1024,256]{1,0:T(8,128)(2,1)S(1)}, f32[1024]{0:T(1024)S(1)}, /*index=5*/s32[]{:T(128)}, s32[]{:T(128)}, s32[]{:T(128)}, s32[]{:T(128)}) while((s32[]{:T(128)}, f32[1024]{0:T(1024)S(1)}, bf16[32768,256]{1,0:T(8,128)(2,1)}, ...), condition=%wide.region_4.5_spmd.clone, body=%wide.region_2.4_spmd.clone.sunk | while | flops 2172650496 | bytes 2642073 | solution.py:32
  94.8 6.6 %fusion.11 = f32[1024]{0:T(1024)S(1)} fusion(bf16[1024,256]{1,0:T(8,128)(2,1)S(1)} %get-tuple-element.192, f32[1024]{0:T(1024)S(1)} %get-tuple-element.193, bf16[32768,256]{1,0:T(8,128)(2,1)} %get-tuple-element.191, s32[]{:T(128)S(6)} %select_n.43), kind=kOutput, calls=%fused_computation.3.clone.1 | convolution fusion | flops 2172648448 | bytes 2629636 | tf_op jit(solution)/shard_map/while/body/eval_jaxpr/dot_general | solution.py:27
  101.4 6.5 %fusion.11 = f32[1024]{0:T(1024)S(1)} fusion(bf16[1024,256]{1,0:T(8,128)(2,1)S(1)} %get-tuple-element.192, f32[1024]{0:T(1024)S(1)} %get-tuple-element.193, bf16[32768,256]{1,0:T(8,128)(2,1)} %get-tuple-element.191, s32[]{:T(128)S(6)} %select_n.43), kind=kOutput, calls=%fused_computation.3.clone.1 | convolution fusion | flops 2172648448 | bytes 2629636 | tf_op jit(solution)/shard_map/while/body/eval_jaxpr/dot_general | solution.py:27
  108.0 6.5 %fusion.11 = f32[1024]{0:T(1024)S(1)} fusion(bf16[1024,256]{1,0:T(8,128)(2,1)S(1)} %get-tuple-element.192, f32[1024]{0:T(1024)S(1)} %get-tuple-element.193, bf16[32768,256]{1,0:T(8,128)(2,1)} %get-tuple-element.191, s32[]{:T(128)S(6)} %select_n.43), kind=kOutput, calls=%fused_computation.3.clone.1 | convolution fusion | flops 2172648448 | bytes 2629636 | tf_op jit(solution)/shard_map/while/body/eval_jaxpr/dot_general | solution.py:27
  114.6 6.5 %fusion.11 = f32[1024]{0:T(1024)S(1)} fusion(bf16[1024,256]{1,0:T(8,128)(2,1)S(1)} %get-tuple-element.192, f32[1024]{0:T(1024)S(1)} %get-tuple-element.193, bf16[32768,256]{1,0:T(8,128)(2,1)} %get-tuple-element.191, s32[]{:T(128)S(6)} %select_n.43), kind=kOutput, calls=%fused_computation.3.clone.1 | convolution fusion | flops 2172648448 | bytes 2629636 | tf_op jit(solution)/shard_map/while/body/eval_jaxpr/dot_general | solution.py:27
  121.2 6.5 %fusion.11 = f32[1024]{0:T(1024)S(1)} fusion(bf16[1024,256]{1,0:T(8,128)(2,1)S(1)} %get-tuple-element.192, f32[1024]{0:T(1024)S(1)} %get-tuple-element.193, bf16[32768,256]{1,0:T(8,128)(2,1)} %get-tuple-element.191, s32[]{:T(128)S(6)} %select_n.43), kind=kOutput, calls=%fused_computation.3.clone.1 | convolution fusion | flops 2172648448 | bytes 2629636 | tf_op jit(solution)/shard_map/while/body/eval_jaxpr/dot_general | solution.py:27
  127.8 6.5 %fusion.11 = f32[1024]{0:T(1024)S(1)} fusion(bf16[1024,256]{1,0:T(8,128)(2,1)S(1)} %get-tuple-element.192, f32[1024]{0:T(1024)S(1)} %get-tuple-element.193, bf16[32768,256]{1,0:T(8,128)(2,1)} %get-tuple-element.191, s32[]{:T(128)S(6)} %select_n.43), kind=kOutput, calls=%fused_computation.3.clone.1 | convolution fusion | flops 2172648448 | bytes 2629636 | tf_op jit(solution)/shard_map/while/body/eval_jaxpr/dot_general | solution.py:27
  134.4 6.5 %fusion.11 = f32[1024]{0:T(1024)S(1)} fusion(bf16[1024,256]{1,0:T(8,128)(2,1)S(1)} %get-tuple-element.192, f32[1024]{0:T(1024)S(1)} %get-tuple-element.193, bf16[32768,256]{1,0:T(8,128)(2,1)} %get-tuple-element.191, s32[]{:T(128)S(6)} %select_n.43), kind=kOutput, calls=%fused_computation.3.clone.1 | convolution fusion | flops 2172648448 | bytes 2629636 | tf_op jit(solution)/shard_map/while/body/eval_jaxpr/dot_general | solution.py:27
  140.9 6.5 %fusion.11 = f32[1024]{0:T(1024)S(1)} fusion(bf16[1024,256]{1,0:T(8,128)(2,1)S(1)} %get-tuple-element.192, f32[1024]{0:T(1024)S(1)} %get-tuple-element.193, bf16[32768,256]{1,0:T(8,128)(2,1)} %get-tuple-element.191, s32[]{:T(128)S(6)} %select_n.43), kind=kOutput, calls=%fused_computation.3.clone.1 | convolution fusion | flops 2172648448 | bytes 2629636 | tf_op jit(solution)/shard_map/while/body/eval_jaxpr/dot_general | solution.py:27
  147.5 17.1 %psum.29 = f32[1024]{0:T(1024)S(1)} all-reduce(f32[1024]{0:T(1024)S(1)} %sub.59), channel_id=1, replica_groups=mesh['items'=8,'users'=4] {'items'}, use_global_device_ids=true, to_apply=%region_6.7 | all-reduce | flops 1024 | bytes 8192 | tf_op jit(solution)/shard_map/psum | solution.py:41
  164.7 0.0 copy-done
  164.7 1.3 divide_reduce_fusion.1
  166.0 6.3 %all-reduce = (f32[1]{0:T(128)}, f32[1]{0:T(128)}) all-reduce(f32[1]{0:T(128)} %bitcast.2, f32[1]{0:T(128)} %bitcast.1), channel_id=1, replica_groups=mesh['items'=8,'users'=4] {'users'}, use_global_device_ids=true, to_apply=%region_11.12 | all-reduce | flops 2 | bytes 16 | tf_op jit(solution)/shard_map/psum | solution.py:46
  172.3 1.8 %maximum_multiply_fusion = f32[2]{0:T(128)} fusion(f32[1]{0:T(128)} %get-tuple-element.137, f32[1]{0:T(128)} %get-tuple-element.138), kind=kLoop, calls=%fused_computation.22 | loop fusion | flops 4 | bytes 16 | tf_op jit(solution)/shard_map/div | solution.py:47
  (15 shorter events, 0.1 us)
Async XLA Ops:
  0.6 24.4 %copy-start.1 = (bf16[1024,32]{0,1:T(8,128)(2,1)S(1)}, bf16[1024,32]{0,1:T(8,128)(2,1)}, u32[]{:S(2)}) copy-start(bf16[1024,32]{0,1:T(8,128)(2,1)} %param.6) | copy-start | bytes 196612
  0.6 60.7 %copy-start.2 = (s32[1024]{0:T(1024)S(1)}, s32[1024]{0:T(1024)}, u32[]{:S(2)}) copy-start(s32[1024]{0:T(1024)} %param.8) | copy-start | bytes 12292
  94.8 69.9 %copy-start = (s32[1024,32]{0,1:T(8,128)S(1)}, s32[1024,32]{0,1:T(8,128)}, u32[]{:S(2)}) copy-start(s32[1024,32]{0,1:T(8,128)} %param.9) | copy-start | bytes 393220
where the time goes:
time: 175 us; the launch traced here: 174 us
  blocking collectives  78 us (45%)
  matrix products  52.4 us (30%)
  local copies, waits for them, and re-layouts  35.5 us (20%)
  other arithmetic  7.14 us (4%)
    dot_general x8, matrix products, add_block(): lax.dot_general(users, rows, (((1,), (1,)), ((), ())), preferred_element_...  52.4 us
    all_gather x1, blocking collectives, body(): users = lax.all_gather(user_emb, 'items', axis=1, tiled=True)  33 us
    gather x2, local copies, waits for them, and re-layouts, body(): hrows = item_emb[own_hist - start]  23 us
    psum x1, blocking collectives, body(): tscore = lax.psum(jnp.where(inside, partial_t, 0.0), 'items')  21.5 us
    psum x1, blocking collectives, body(): above = lax.psum(local, 'items') - correction  17.1 us
    gather x1, local copies, waits for them, and re-layouts, body(): own_rows = item_emb[jnp.clip(local_t, 0, item_dev - 1)]  11.4 us
    psum x1, blocking collectives, body(): hit_sum, gain_sum = lax.psum((jnp.sum(hit), jnp.sum(gain)), 'users')  6.3 us

commit v1 on v0

--- a/solution.py
+++ b/solution.py
@@ -2,6 +2,7 @@
 import jax.numpy as jnp
 from jax import lax
 from jax.sharding import PartitionSpec as P
+from jax.lax import axis_index, axis_size, ppermute
 
 sharpness = 4.0
 
@@ -13,7 +14,25 @@
     local_t = target - start
     inside = (local_t >= 0) & (local_t < item_dev)
     own_rows = item_emb[jnp.clip(local_t, 0, item_dev - 1)]
-    users = lax.all_gather(user_emb, "items", axis=1, tiled=True)
+
+    def solve_the_pools(local_block, axis_tag):
+        chips = axis_size(axis_tag)
+        series = [(at, (at + 1) % chips) for at in range(chips)]
+
+        def _extend_blocks(all_values):
+            if len(all_values) == chips:
+                return all_values
+            x_new = ppermute(all_values[0], axis_name=axis_tag, perm=series)
+            later = _extend_blocks([x_new, *all_values])
+            return later
+
+        t1 = _extend_blocks([local_block])
+        outer = jnp.concatenate(t1, axis=1)
+        earlier = axis_index(axis_tag)
+        y = jnp.roll(outer, (earlier + 1) * local_block.shape[1], axis=1)
+        return y
+
+    users = solve_the_pools(user_emb, "items")
     partial_t = jnp.sum(users.astype(jnp.float32) * own_rows.astype(jnp.float32), axis=1)
     tscore = lax.psum(jnp.where(inside, partial_t, 0.0), "items")
     n_items = lax.axis_size("items")

time: 175 us -> 211 us (1.21)
  waiting for transfers between devices: 0 us -> 54.6 us
  blocking collectives: 78 us -> 42.6 us
  local copies, waits for them, and re-layouts: 35.5 us -> 46 us
  starting transfers between devices: 0 us -> 3.06 us
  matrix products: 52.4 us -> 55.1 us
    ppermute x0 -> x7, waiting for transfers between devices: none -> 54.6 us  [_extend_blocks(): x_new = ppermute(all_values[0], axis_name=axis_tag, perm=series)]
    all_gather x1 -> x0, blocking collectives: 33 us -> none  [body(): users = lax.all_gather(user_emb, 'items', axis=1, tiled=True)]
    concatenate x0 -> x1, local copies, waits for them, and re-layouts: none -> 5.06 us  [solve_the_pools(): y = jnp.roll(outer, (earlier + 1) * local_block.shape[1], axis=1)]
    while x0 -> x32, local copies, waits for them, and re-layouts: none -> 4.7 us
    ppermute x0 -> x7, starting transfers between devices: none -> 3.06 us  [_extend_blocks(): x_new = ppermute(all_values[0], axis_name=axis_tag, perm=series)]
    unnamed x2 -> x1, other arithmetic: 2.91 us -> 0.01 us
    dot_general x0 -> x1, matrix products: none -> 2.81 us  [body(): jnp.einsum('ud,uhd->uh', users, hrows, preferred_element_type=jnp.float32)]
    psum x1, blocking collectives: 21.5 us -> 19.2 us  [body(): tscore = lax.psum(jnp.where(inside, partial_t, 0.0), 'items')]
  transfers between devices with their start and end apart: 0 -> 7, of which waited for: 0 -> 6; matrix products, arithmetic and copies ran while one was open for 0% -> 18% of each run, Pallas kernels for 0% -> 0%
where the time goes in v1:
time: 211 us; the launch traced here: 210 us
  matrix products  55.1 us (26%)
  waiting for transfers between devices  54.6 us (26%)
  local copies, waits for them, and re-layouts  46 us (22%)
  blocking collectives  42.6 us (20%)
  other arithmetic  7.4 us (4%)
  starting transfers between devices  3.06 us (1%)
    ppermute x7, waiting for transfers between devices, _extend_blocks(): x_new = ppermute(all_values[0], axis_name=axis_tag, perm=series)  54.6 us
    dot_general x8, matrix products, add_block(): lax.dot_general(users, rows, (((1,), (1,)), ((), ())), preferred_element_...  52.3 us
    gather x2, local copies, waits for them, and re-layouts, body(): hrows = item_emb[own_hist - start]  23 us
    psum x1, blocking collectives, body(): tscore = lax.psum(jnp.where(inside, partial_t, 0.0), 'items')  19.2 us
    psum x1, blocking collectives, body(): above = lax.psum(local, 'items') - correction  17.1 us
    gather x1, local copies, waits for them, and re-layouts, body(): own_rows = item_emb[jnp.clip(local_t, 0, item_dev - 1)]  11.4 us
    psum x1, blocking collectives, body(): hit_sum, gain_sum = lax.psum((jnp.sum(hit), jnp.sum(gain)), 'users')  6.3 us
    concatenate x1, local copies, waits for them, and re-layouts, solve_the_pools(): y = jnp.roll(outer, (earlier + 1) * local_block.shape[1], axis=1)  5.06 us
  transfers between devices with their start and end apart: 7, of which 6 were waited for; matrix products, arithmetic and copies ran while one was open for 18% of the time, Pallas kernels for 0%

profile of v1, /device:TPU:0, one launch (start us, length us, event | category | flops | bytes accessed | tf_op | source)
XLA Modules:
  0.0 209.8 jit_solution(5084373364069518410)
XLA Ops:
  0.6 0.0 copy-start.1
  0.6 1.0 copy.13
  1.7 3.0 %collective-permute-start = (bf16[1024,32]{1,0:T(8,128)(2,1)S(1)}, bf16[1024,32]{1,0:T(8,128)(2,1)S(1)}, u32[]{:S(2)}, u32[]{:S(2)}) collective-permute-start(bf16[1024,32]{1,0:T(8,128)(2,1)S(1)} %copy.13), channel_id=1, source_target_pairs={{0,4},{4,8},{8,12},{12,16},{16,20},{20,24},{24,28},{28,0},{1,5},{5... | collective-permute-start | bytes 196616 | tf_op jit(solution)/shard_map/ppermute | solution.py:25
  4.7 9.3 %collective-permute-done = bf16[1024,32]{1,0:T(8,128)(2,1)S(1)} collective-permute-done((bf16[1024,32]{1,0:T(8,128)(2,1)S(1)}, bf16[1024,32]{1,0:T(8,128)(2,1)S(1)}, u32[]{:S(2)}, u32[]{:S(2)}) %collective-permute-start) | collective-permute-done | bytes 65568 | tf_op jit(solution)/shard_map/ppermute | solution.py:25
  14.1 0.0 collective-permute-start.1
  14.1 10.2 %collective-permute-done.1 = bf16[1024,32]{1,0:T(8,128)(2,1)S(1)} collective-permute-done((bf16[1024,32]{1,0:T(8,128)(2,1)S(1)}, bf16[1024,32]{1,0:T(8,128)(2,1)S(1)}, u32[]{:S(2)}, u32[]{:S(2)}) %collective-permute-start.1) | collective-permute-done | bytes 65568 | tf_op jit(solution)/shard_map/ppermute | solution.py:25
  24.2 0.0 collective-permute-start.2
  24.3 9.3 %collective-permute-done.2 = bf16[1024,32]{1,0:T(8,128)(2,1)S(1)} collective-permute-done((bf16[1024,32]{1,0:T(8,128)(2,1)S(1)}, bf16[1024,32]{1,0:T(8,128)(2,1)S(1)}, u32[]{:S(2)}, u32[]{:S(2)}) %collective-permute-start.2) | collective-permute-done | bytes 65568 | tf_op jit(solution)/shard_map/ppermute | solution.py:25
  33.6 0.0 collective-permute-start.3
  33.6 0.8 compare_select_fusion
  34.4 0.2 copy.16
  34.6 0.3 reshape.17
  34.9 7.9 %collective-permute-done.3 = bf16[1024,32]{1,0:T(8,128)(2,1)} collective-permute-done((bf16[1024,32]{1,0:T(8,128)(2,1)S(1)}, bf16[1024,32]{1,0:T(8,128)(2,1)}, u32[]{:S(2)}, u32[]{:S(2)}) %collective-permute-start.3) | collective-permute-done | bytes 65568 | tf_op jit(solution)/shard_map/ppermute | solution.py:25
  42.7 0.0 collective-permute-start.4
  42.7 9.4 %collective-permute-done.4 = bf16[1024,32]{1,0:T(8,128)(2,1)} collective-permute-done((bf16[1024,32]{1,0:T(8,128)(2,1)}, bf16[1024,32]{1,0:T(8,128)(2,1)}, u32[]{:S(2)}, u32[]{:S(2)}) %collective-permute-start.4) | collective-permute-done | bytes 65568 | tf_op jit(solution)/shard_map/ppermute | solution.py:25
  52.1 0.0 collective-permute-start.5
  52.1 0.7 fusion.11
  52.8 11.4 %gather_fusion = bf16[1024,256]{1,0:T(8,128)(2,1)S(1)} fusion(bf16[32768,256]{1,0:T(8,128)(2,1)} %param.7, s32[1024]{0:T(1024)S(1)} %fusion.11), kind=kCustom, calls=%fused_computation | custom fusion | bytes 1052672 | tf_op jit(solution)/shard_map/gather | solution.py:16
  64.2 20.9 %gather_fusion.1 = bf16[4096,256]{1,0:T(8,128)(2,1)S(1)} fusion(bf16[32768,256]{1,0:T(8,128)(2,1)} %param.7, s32[4096]{0:T(1024)S(1)} %broadcast_clamp_fusion), kind=kCustom, calls=%fused_computation.1 | custom fusion | bytes 4210688 | tf_op jit(solution)/shard_map/gather | solution.py:54
  85.2 2.1 reshape.16
  87.2 0.0 collective-permute-done.5
  87.2 0.0 collective-permute-start.6
  87.3 0.0 copy-done.1
  87.3 0.7 compare_reduce_fusion
  88.0 8.6 %collective-permute-done.6 = bf16[1024,32]{1,0:T(8,128)(2,1)S(1)} collective-permute-done((bf16[1024,32]{1,0:T(8,128)(2,1)}, bf16[1024,32]{1,0:T(8,128)(2,1)S(1)}, u32[]{:S(2)}, u32[]{:S(2)}) %collective-permute-start.6) | collective-permute-done | bytes 65568 | tf_op jit(solution)/shard_map/ppermute | solution.py:25
  96.5 5.1 %concatenate.6 = bf16[1024,512]{1,0:T(8,128)(2,1)S(1)} concatenate(bf16[1024,32]{1,0:T(8,128)(2,1)S(1)} %collective-permute-done.6, bf16[1024,32]{1,0:T(8,128)(2,1)} %collective-permute-done.5, bf16[1024,32]{1,0:T(8,128)(2,1)} %collective-permute-done.4, bf16[1024,32]{1,0:T(8,128)(2,1)} %collective-permute-done.3, bf16[1024,32]{1,0:T(8,128)(2,1)} %copy-done, ...), dimensions={1} | concatenate | bytes 2097152 | tf_op jit(solution)/shard_map/jit(_roll_dynamic)/concatenate | solution.py:32
  101.6 0.7 multiply_reduce_fusion
  102.2 2.8 %fusion.3 = f32[1024,1,4]{2,1,0:T(1,128)S(1)} fusion(bf16[1024,4,256]{2,1,0:T(4,128)(2,1)} %reshape.16, bf16[1024,256,1]{1,0,2:T(8,128)(2,1)S(1)} %bitcast.21), kind=kOutput, calls=%fused_computation.8 | convolution fusion | flops 2097152 | bytes 2637824 | tf_op jit(solution)/shard_map/ud,uhd->uh/dot_general | solution.py:55
  105.1 0.3 copy.18
  105.3 0.7 and_select_fusion
  106.1 19.2 %psum.28 = f32[1024]{0:T(1024)S(1)} all-reduce(f32[1024]{0:T(1024)S(1)} %and_select_fusion), channel_id=1, replica_groups=mesh['items'=8,'users'=4] {'items'}, use_global_device_ids=true, to_apply=%region_1.2 | all-reduce | flops 1024 | bytes 8192 | tf_op jit(solution)/shard_map/psum | solution.py:37
  125.2 57.4 %while.14 = (s32[]{:T(128)}, f32[1024]{0:T(1024)}, bf16[32768,256]{1,0:T(8,128)(2,1)}, bf16[1024,256]{1,0:T(8,128)(2,1)S(1)}, f32[1024]{0:T(1024)S(1)}, /*index=5*/s32[]{:T(128)}, s32[]{:T(128)}, s32[]{:T(128)}, s32[]{:T(128)}) while((s32[]{:T(128)}, f32[1024]{0:T(1024)}, bf16[32768,256]{1,0:T(8,128)(2,1)}, ...), condition=%wide.region_4.5_spmd.clone, body=%wide.region_2.4_spmd.clone.sunk | while | flops 2172650496 | bytes 2674897 | solution.py:51
  125.3 0.0 copy-start.2
  125.3 6.5 %fusion.19 = f32[1024]{0:T(1024)S(1)} fusion(bf16[1024,256]{1,0:T(8,128)(2,1)S(1)} %get-tuple-element.184, f32[1024]{0:T(1024)S(1)} %get-tuple-element.185, bf16[32768,256]{1,0:T(8,128)(2,1)} %get-tuple-element.183, s32[]{:T(128)S(6)} %select_n.58), kind=kOutput, calls=%fused_computation.3.clone.1 | convolution fusion | flops 2172648448 | bytes 2629636 | tf_op jit(solution)/shard_map/while/body/eval_jaxpr/dot_general | solution.py:46
  131.9 0.0 copy-start.3
  131.9 0.6 copy-done.3
  132.5 6.5 %fusion.19 = f32[1024]{0:T(1024)S(1)} fusion(bf16[1024,256]{1,0:T(8,128)(2,1)S(1)} %get-tuple-element.184, f32[1024]{0:T(1024)S(1)} %get-tuple-element.185, bf16[32768,256]{1,0:T(8,128)(2,1)} %get-tuple-element.183, s32[]{:T(128)S(6)} %select_n.58), kind=kOutput, calls=%fused_computation.3.clone.1 | convolution fusion | flops 2172648448 | bytes 2629636 | tf_op jit(solution)/shard_map/while/body/eval_jaxpr/dot_general | solution.py:46
  139.0 0.0 copy-start.3
  139.0 0.6 copy-done.3
  139.6 6.5 %fusion.19 = f32[1024]{0:T(1024)S(1)} fusion(bf16[1024,256]{1,0:T(8,128)(2,1)S(1)} %get-tuple-element.184, f32[1024]{0:T(1024)S(1)} %get-tuple-element.185, bf16[32768,256]{1,0:T(8,128)(2,1)} %get-tuple-element.183, s32[]{:T(128)S(6)} %select_n.58), kind=kOutput, calls=%fused_computation.3.clone.1 | convolution fusion | flops 2172648448 | bytes 2629636 | tf_op jit(solution)/shard_map/while/body/eval_jaxpr/dot_general | solution.py:46
  146.2 0.0 copy-start.3
  146.2 0.6 copy-done.3
  146.8 6.5 %fusion.19 = f32[1024]{0:T(1024)S(1)} fusion(bf16[1024,256]{1,0:T(8,128)(2,1)S(1)} %get-tuple-element.184, f32[1024]{0:T(1024)S(1)} %get-tuple-element.185, bf16[32768,256]{1,0:T(8,128)(2,1)} %get-tuple-element.183, s32[]{:T(128)S(6)} %select_n.58), kind=kOutput, calls=%fused_computation.3.clone.1 | convolution fusion | flops 2172648448 | bytes 2629636 | tf_op jit(solution)/shard_map/while/body/eval_jaxpr/dot_general | solution.py:46
  153.3 0.0 copy-done.2
  153.4 0.0 copy-start.3
  153.4 0.6 copy-done.3
  154.0 6.5 %fusion.19 = f32[1024]{0:T(1024)S(1)} fusion(bf16[1024,256]{1,0:T(8,128)(2,1)S(1)} %get-tuple-element.184, f32[1024]{0:T(1024)S(1)} %get-tuple-element.185, bf16[32768,256]{1,0:T(8,128)(2,1)} %get-tuple-element.183, s32[]{:T(128)S(6)} %select_n.58), kind=kOutput, calls=%fused_computation.3.clone.1 | convolution fusion | flops 2172648448 | bytes 2629636 | tf_op jit(solution)/shard_map/while/body/eval_jaxpr/dot_general | solution.py:46
  160.5 0.0 copy-start.3
  160.5 0.6 copy-done.3
  161.1 6.5 %fusion.19 = f32[1024]{0:T(1024)S(1)} fusion(bf16[1024,256]{1,0:T(8,128)(2,1)S(1)} %get-tuple-element.184, f32[1024]{0:T(1024)S(1)} %get-tuple-element.185, bf16[32768,256]{1,0:T(8,128)(2,1)} %get-tuple-element.183, s32[]{:T(128)S(6)} %select_n.58), kind=kOutput, calls=%fused_computation.3.clone.1 | convolution fusion | flops 2172648448 | bytes 2629636 | tf_op jit(solution)/shard_map/while/body/eval_jaxpr/dot_general | solution.py:46
  167.7 0.0 copy-start.3
  167.7 0.6 copy-done.3
  168.3 6.5 %fusion.19 = f32[1024]{0:T(1024)S(1)} fusion(bf16[1024,256]{1,0:T(8,128)(2,1)S(1)} %get-tuple-element.184, f32[1024]{0:T(1024)S(1)} %get-tuple-element.185, bf16[32768,256]{1,0:T(8,128)(2,1)} %get-tuple-element.183, s32[]{:T(128)S(6)} %select_n.58), kind=kOutput, calls=%fused_computation.3.clone.1 | convolution fusion | flops 2172648448 | bytes 2629636 | tf_op jit(solution)/shard_map/while/body/eval_jaxpr/dot_general | solution.py:46
  174.9 0.0 copy-start.3
  174.9 0.6 copy-done.3
  175.5 6.5 %fusion.19 = f32[1024]{0:T(1024)S(1)} fusion(bf16[1024,256]{1,0:T(8,128)(2,1)S(1)} %get-tuple-element.184, f32[1024]{0:T(1024)S(1)} %get-tuple-element.185, bf16[32768,256]{1,0:T(8,128)(2,1)} %get-tuple-element.183, s32[]{:T(128)S(6)} %select_n.58), kind=kOutput, calls=%fused_computation.3.clone.1 | convolution fusion | flops 2172648448 | bytes 2629636 | tf_op jit(solution)/shard_map/while/body/eval_jaxpr/dot_general | solution.py:46
  182.0 0.0 copy-done.2
  182.0 0.0 copy-start.3
  182.0 0.6 copy-done.3
  182.6 0.7 sub.64
  183.3 17.1 %psum.29 = f32[1024]{0:T(1024)S(1)} all-reduce(f32[1024]{0:T(1024)S(1)} %sub.64), channel_id=1, replica_groups=mesh['items'=8,'users'=4] {'items'}, use_global_device_ids=true, to_apply=%region_6.7 | all-reduce | flops 1024 | bytes 8192 | tf_op jit(solution)/shard_map/psum | solution.py:60
  200.4 1.3 divide_reduce_fusion.1
  201.7 6.3 %all-reduce = (f32[1]{0:T(128)}, f32[1]{0:T(128)}) all-reduce(f32[1]{0:T(128)} %bitcast.3, f32[1]{0:T(128)} %bitcast.2), channel_id=1, replica_groups=mesh['items'=8,'users'=4] {'users'}, use_global_device_ids=true, to_apply=%region_11.12 | all-reduce | flops 2 | bytes 16 | tf_op jit(solution)/shard_map/psum | solution.py:65
  208.0 1.8 maximum_multiply_fusion
  (26 shorter events, 0.1 us)
Async XLA Ops:
  0.6 86.6 %copy-start.1 = (s32[1024,32]{0,1:T(8,128)S(1)}, s32[1024,32]{0,1:T(8,128)}, u32[]{:S(2)}) copy-start(s32[1024,32]{0,1:T(8,128)} %param.9) | copy-start | bytes 393220
  1.7 12.4 %collective-permute-start = (bf16[1024,32]{1,0:T(8,128)(2,1)S(1)}, bf16[1024,32]{1,0:T(8,128)(2,1)S(1)}, u32[]{:S(2)}, u32[]{:S(2)}) collective-permute-start(bf16[1024,32]{1,0:T(8,128)(2,1)S(1)} %copy.13), channel_id=1, source_target_pairs={{0,4},{4,8},{8,12},{12,16},{16,20},{20,24},{24,28},{28,0},{1,5},{5... | collective-permute-start | bytes 196616 | tf_op jit(solution)/shard_map/ppermute | solution.py:25
  14.1 10.2 %collective-permute-start.1 = (bf16[1024,32]{1,0:T(8,128)(2,1)S(1)}, bf16[1024,32]{1,0:T(8,128)(2,1)S(1)}, u32[]{:S(2)}, u32[]{:S(2)}) collective-permute-start(bf16[1024,32]{1,0:T(8,128)(2,1)S(1)} %collective-permute-done), channel_id=1, source_target_pairs={{0,4},{4,8},{8,12},{12,16},{16,20},{20,24},{24,28},{28,0},{1,5},{5... | collective-permute-start | bytes 196616 | tf_op jit(solution)/shard_map/ppermute | solution.py:25
  24.2 9.3 %collective-permute-start.2 = (bf16[1024,32]{1,0:T(8,128)(2,1)S(1)}, bf16[1024,32]{1,0:T(8,128)(2,1)S(1)}, u32[]{:S(2)}, u32[]{:S(2)}) collective-permute-start(bf16[1024,32]{1,0:T(8,128)(2,1)S(1)} %collective-permute-done.1), channel_id=1, source_target_pairs={{0,4},{4,8},{8,12},{12,16},{16,20},{20,24},{24,28},{28,0},{1,5},{5... | collective-permute-start | bytes 196616 | tf_op jit(solution)/shard_map/ppermute | solution.py:25
  33.6 19.3 %copy-start = (bf16[1024,32]{1,0:T(8,128)(2,1)}, bf16[1024,32]{1,0:T(8,128)(2,1)S(1)}, u32[]{:S(2)}) copy-start(bf16[1024,32]{1,0:T(8,128)(2,1)S(1)} %collective-permute-done.2) | copy-start | bytes 196612
  33.6 9.2 %collective-permute-start.3 = (bf16[1024,32]{1,0:T(8,128)(2,1)S(1)}, bf16[1024,32]{1,0:T(8,128)(2,1)}, u32[]{:S(2)}, u32[]{:S(2)}) collective-permute-start(bf16[1024,32]{1,0:T(8,128)(2,1)S(1)} %collective-permute-done.2), channel_id=1, source_target_pairs={{0,4},{4,8},{8,12},{12,16},{16,20},{20,24},{24,28},{28,0},{1,5},{5... | collective-permute-start | bytes 196616 | tf_op jit(solution)/shard_map/ppermute | solution.py:25
  42.7 9.4 %collective-permute-start.4 = (bf16[1024,32]{1,0:T(8,128)(2,1)}, bf16[1024,32]{1,0:T(8,128)(2,1)}, u32[]{:S(2)}, u32[]{:S(2)}) collective-permute-start(bf16[1024,32]{1,0:T(8,128)(2,1)} %collective-permute-done.3), channel_id=1, source_target_pairs={{0,4},{4,8},{8,12},{12,16},{16,20},{20,24},{24,28},{28,0},{1,5},{5... | collective-permute-start | bytes 196616 | tf_op jit(solution)/shard_map/ppermute | solution.py:25
  52.1 35.1 %collective-permute-start.5 = (bf16[1024,32]{1,0:T(8,128)(2,1)}, bf16[1024,32]{1,0:T(8,128)(2,1)}, u32[]{:S(2)}, u32[]{:S(2)}) collective-permute-start(bf16[1024,32]{1,0:T(8,128)(2,1)} %collective-permute-done.4), channel_id=1, source_target_pairs={{0,4},{4,8},{8,12},{12,16},{16,20},{20,24},{24,28},{28,0},{1,5},{5... | collective-permute-start | bytes 196616 | tf_op jit(solution)/shard_map/ppermute | solution.py:25
  87.2 9.3 %collective-permute-start.6 = (bf16[1024,32]{1,0:T(8,128)(2,1)}, bf16[1024,32]{1,0:T(8,128)(2,1)S(1)}, u32[]{:S(2)}, u32[]{:S(2)}) collective-permute-start(bf16[1024,32]{1,0:T(8,128)(2,1)} %collective-permute-done.5), channel_id=1, source_target_pairs={{0,4},{4,8},{8,12},{12,16},{16,20},{20,24},{24,28},{28,0},{1,5},{5... | collective-permute-start | bytes 196616 | tf_op jit(solution)/shard_map/ppermute | solution.py:25
  125.3 6.6 %copy-start.2 = (f32[1024]{0:T(1024)S(1)}, f32[1024]{0:T(1024)}, u32[]{:S(2)}) copy-start(f32[1024]{0:T(1024)} %get-tuple-element.173) | copy-start | bytes 12292 | tf_op jit(solution)/shard_map/while
  131.9 0.6 copy-start.3
  132.5 6.5 %copy-start.2 = (f32[1024]{0:T(1024)S(1)}, f32[1024]{0:T(1024)}, u32[]{:S(2)}) copy-start(f32[1024]{0:T(1024)} %get-tuple-element.173) | copy-start | bytes 12292 | tf_op jit(solution)/shard_map/while
  139.0 0.6 copy-start.3
  139.6 6.5 %copy-start.2 = (f32[1024]{0:T(1024)S(1)}, f32[1024]{0:T(1024)}, u32[]{:S(2)}) copy-start(f32[1024]{0:T(1024)} %get-tuple-element.173) | copy-start | bytes 12292 | tf_op jit(solution)/shard_map/while
  146.2 0.6 copy-start.3
  146.8 6.5 %copy-start.2 = (f32[1024]{0:T(1024)S(1)}, f32[1024]{0:T(1024)}, u32[]{:S(2)}) copy-start(f32[1024]{0:T(1024)} %get-tuple-element.173) | copy-start | bytes 12292 | tf_op jit(solution)/shard_map/while
  153.4 0.6 copy-start.3
  154.0 6.5 %copy-start.2 = (f32[1024]{0:T(1024)S(1)}, f32[1024]{0:T(1024)}, u32[]{:S(2)}) copy-start(f32[1024]{0:T(1024)} %get-tuple-element.173) | copy-start | bytes 12292 | tf_op jit(solution)/shard_map/while
  160.5 0.6 copy-start.3
  161.1 6.5 %copy-start.2 = (f32[1024]{0:T(1024)S(1)}, f32[1024]{0:T(1024)}, u32[]{:S(2)}) copy-start(f32[1024]{0:T(1024)} %get-tuple-element.173) | copy-start | bytes 12292 | tf_op jit(solution)/shard_map/while
  167.7 0.6 copy-start.3
  168.3 6.5 %copy-start.2 = (f32[1024]{0:T(1024)S(1)}, f32[1024]{0:T(1024)}, u32[]{:S(2)}) copy-start(f32[1024]{0:T(1024)} %get-tuple-element.173) | copy-start | bytes 12292 | tf_op jit(solution)/shard_map/while
  174.9 0.6 copy-start.3
  175.5 6.5 %copy-start.2 = (f32[1024]{0:T(1024)S(1)}, f32[1024]{0:T(1024)}, u32[]{:S(2)}) copy-start(f32[1024]{0:T(1024)} %get-tuple-element.173) | copy-start | bytes 12292 | tf_op jit(solution)/shard_map/while
  182.0 0.6 copy-start.3
